TPU v7x, 128 devices: a whole 4x4x4 slice. The times are simulated.
128 devices in a mesh: seq: 16 (over z_hi, y, core), tensor: 8 (over z_lo, x).
Axes of the slice: x: 4, y: 4, z: 4 (z_hi: 2, z_lo: 2; z = z_hi * 2 + z_lo), core: 2. Of those that a mesh axis runs over, the one named last changes fastest.
Arguments:
- tokens: bfloat16 [11520, 1536], P('seq'), may hold values from -6 to 6
- norm_gain: float32 [1536], replicated, may hold values from 0.1 to 1.9
- w_qkv: bfloat16 [1536, 3, 1536], P(None, None, 'tensor'), may hold values from -8 to 8
- w_out: bfloat16 [1536, 1536], P('tensor'), may hold values from -0.15625 to 0.15625
- post_gain: float32 [1536], replicated, may hold values from 0.1 to 1.9
- w_up: bfloat16 [1536, 6144], P(None, 'tensor'), may hold values from -0.15625 to 0.15625
- w_down: bfloat16 [6144, 1536], P('tensor'), may hold values from -0.078125 to 0.078125
Outputs:
- layer_out: bfloat16 [11520, 1536], P('seq')
All inputs are finite; a program needn't handle non-finite values.
Results may differ from a plain program's by a relative error of at most 0.015.
Values may be sent and summed in bfloat16 or wider, within the bound.
A program may use at most 128 MiB of HBM per device.

v0:
```python
import jax
import jax.numpy as jnp
from jax import lax
from jax.sharding import PartitionSpec as P

HD = 48


def layer_norm(values, gain):
    mean = jnp.mean(values, axis=-1, keepdims=True)
    centred = values - mean
    var = jnp.mean(centred * centred, axis=-1, keepdims=True)
    return centred * lax.rsqrt(var + 1e-05) * gain


def attend_block(carry, queries, key_rows, value_rows, scale):
    peak, total, accum = carry
    heads = queries.shape[1]
    keys = key_rows.reshape(key_rows.shape[0], heads, -1)
    values = value_rows.reshape(value_rows.shape[0], heads, -1)
    scores = jnp.einsum("qhd,khd->hqk", queries, keys, preferred_element_type=jnp.float32) * scale
    fresh = jnp.maximum(peak, jnp.max(scores, axis=-1))
    factor = jnp.exp(peak - fresh)
    weights = jnp.exp(scores - fresh[..., None])
    total = total * factor + jnp.sum(weights, axis=-1)
    accum = accum * factor[..., None] + jnp.einsum(
        "hqk,khd->hqd", weights.astype(jnp.bfloat16), values, preferred_element_type=jnp.float32
    )
    return (fresh, total, accum)


def empty_state(rows, heads, width):
    return (
        jnp.full((heads, rows), -1e30, jnp.float32),
        jnp.zeros((heads, rows), jnp.float32),
        jnp.zeros((heads, rows, width), jnp.float32),
    )


def per_device(tokens, norm_gain, w_qkv, w_out, post_gain, w_up, w_down):
    rows = tokens.shape[0]
    local_heads = w_qkv.shape[2] // HD
    scale = 1.0 / HD**0.5
    base = tokens.astype(jnp.float32)
    normed = layer_norm(base, norm_gain).astype(jnp.bfloat16)
    qkv = jnp.dot(
        normed, w_qkv.reshape(w_qkv.shape[0], -1), preferred_element_type=jnp.float32
    ).astype(jnp.bfloat16)
    span = local_heads * HD
    query = qkv[:, :span]
    key = qkv[:, span : 2 * span]
    value = qkv[:, 2 * span :]
    query3 = query.reshape(rows, local_heads, HD)
    key_piece = lax.all_gather(key, "seq", axis=0, tiled=True)
    value_piece = lax.all_gather(value, "seq", axis=0, tiled=True)
    count = key_piece.shape[0]
    block = count
    while block > 1024 and block % 2 == 0:
        block = block // 2

    def step(index, state):
        first = index * block
        key_block = lax.dynamic_slice_in_dim(key_piece, first, block, 0)
        value_block = lax.dynamic_slice_in_dim(value_piece, first, block, 0)
        return attend_block(state, query3, key_block, value_block, scale)

    peak, total, accum = lax.fori_loop(0, count // block, step, empty_state(rows, local_heads, HD))
    result = accum / total[..., None]
    attended = jnp.transpose(result, (1, 0, 2)).reshape(rows, span).astype(jnp.bfloat16)
    attn_term = jnp.dot(attended, w_out, preferred_element_type=jnp.float32)
    mixed = base + lax.psum(attn_term.astype(jnp.bfloat16), "tensor").astype(jnp.float32)
    post = layer_norm(mixed, post_gain).astype(jnp.bfloat16)
    hidden = jax.nn.gelu(
        jnp.dot(post, w_up, preferred_element_type=jnp.float32), approximate=True
    ).astype(jnp.bfloat16)
    mlp_term = jnp.dot(hidden, w_down, preferred_element_type=jnp.float32)
    return (mixed + lax.psum(mlp_term.astype(jnp.bfloat16), "tensor").astype(jnp.float32)).astype(
        jnp.bfloat16
    )


def solution(mesh):
    placed = (
        P("seq", None),
        P(),
        P(None, None, "tensor"),
        P("tensor", None),
        P(),
        P(None, "tensor"),
        P("tensor", None),
    )
    return jax.shard_map(
        per_device, mesh=mesh, in_specs=placed, out_specs=P("seq", None), check_vma=False
    )
```

profile of v0, /device:TPU:0, one launch (start us, length us, event | category | flops | bytes accessed | tf_op | source)
XLA Modules:
  0.0 440.2 jit_solution(4622972025881850253)
XLA Ops:
  6.6 2.1 convert_reduce_fusion
  8.7 2.4 fusion.12
  11.2 1.7 fusion.33
  14.6 60.0 %all-gather.7.cloned.1.call-done = bf16[16,720,192]{1,2,0:T(8,128)(2,1)} async-done(((bf16[1,720,192]{1,2,0:T(8,128)(2,1)}), bf16[16,720,192]{1,2,0:T(8,128)(2,1)}) %all-gather.7.cloned.1.call-update) | async-done | bytes 4423696 | tf_op jit(solution)/shard_map/all_gather | solution.py:55
  74.6 7.2 %copy.14 = bf16[16,720,192]{1,0,2:T(8,128)(2,1)} copy(bf16[16,720,192]{1,2,0:T(8,128)(2,1)} %all-gather.7.cloned.1.call-done) | data formatting | bytes 8847360 | tf_op jit(solution)/shard_map/all_gather | solution.py:55
  81.8 10.3 %reshape.56 = bf16[11520,192]{0,1:T(8,128)(2,1)} reshape(bf16[16,720,192]{1,0,2:T(8,128)(2,1)} %copy.14) | data formatting | bytes 8847360
  92.1 41.7 %all-gather.5.cloned.1.call-done = bf16[16,720,192]{1,2,0:T(8,128)(2,1)} async-done(((bf16[1,720,192]{1,2,0:T(8,128)(2,1)}), bf16[16,720,192]{1,2,0:T(8,128)(2,1)}) %all-gather.5.cloned.1.call-update) | async-done | bytes 4423696 | tf_op jit(solution)/shard_map/all_gather | solution.py:54
  133.8 7.1 %copy.13 = bf16[16,720,192]{1,0,2:T(8,128)(2,1)} copy(bf16[16,720,192]{1,2,0:T(8,128)(2,1)} %all-gather.5.cloned.1.call-done) | data formatting | bytes 8847360 | tf_op jit(solution)/shard_map/all_gather | solution.py:54
  140.9 10.2 %reshape.54 = bf16[11520,192]{0,1:T(8,128)(2,1)} reshape(bf16[16,720,192]{1,0,2:T(8,128)(2,1)} %copy.13) | data formatting | bytes 8847360
  151.1 96.1 %while.18 = (s32[]{:T(128)}, f32[4,720]{1,0:T(4,128)S(1)}, f32[4,720]{1,0:T(4,128)S(1)}, f32[4,720,48]{1,2,0:T(8,128)S(1)}, bf16[11520,192]{0,1:T(8,128)(2,1)}, ...) while((s32[]{:T(128)}, f32[4,720]{1,0:T(4,128)S(1)}, ...), condition=%wide.region_5.0_spmd.clone, body=%wide.region_2.0_spmd.clone.sunk | while | flops 415149120 | bytes 28108976 | solution.py:67
  155.4 1.7 fusion.61
  161.4 1.7 fusion.61
  167.4 1.7 fusion.61
  173.4 1.7 fusion.61
  179.4 1.7 fusion.61
  185.4 1.7 fusion.61
  191.4 1.7 fusion.61
  197.5 1.7 fusion.61
  203.5 1.7 fusion.61
  209.5 1.7 fusion.61
  215.5 1.7 fusion.61
  221.5 1.7 fusion.61
  227.5 1.7 fusion.61
  233.5 1.7 fusion.61
  239.5 1.7 fusion.61
  245.5 1.7 fusion.61
  247.3 3.2 convolution_convert_fusion.1
  250.8 81.1 %all-reduce.3.cloned.1.call-done = bf16[720,1536]{1,0:T(8,128)(2,1)} async-done(((bf16[720,1536]{1,0:T(8,128)(2,1)}), bf16[720,1536]{1,0:T(8,128)(2,1)}) %all-reduce.3.cloned.1.call-update) | async-done | bytes 2211856 | tf_op jit(solution)/shard_map/psum | solution.py:71
  331.9 3.1 fusion.15
  336.5 8.9 %convolution_convert_fusion = bf16[720,1536]{1,0:T(8,128)(2,1)} fusion(bf16[768,1536]{1,0:T(8,128)(2,1)S(1)} %copy-done, bf16[1536,768]{1,0:T(8,128)(2,1)} %param.14, bf16[720,1536]{1,0:T(8,128)(2,1)} %all-reduce.3.cloned.1.call-done, bf16[720,1536]{1,0:T(8,128)(2,1)} %param.9, f32[1536]{0:T(1024)S(1)} %copy-done.6, f32[720]{0:T(1024)S(1)} %add_rsqrt_fusion, ...), kind=kOutput, calls=%fused_computation.28 | convolution fusion | flops 3411210240 | bytes 11366016 | tf_op jit(solution)/shard_map/dot_general | solution.py:76
  345.4 83.1 %all-reduce.5.cloned.1.call-done = bf16[720,1536]{1,0:T(8,128)(2,1)} async-done(((bf16[720,1536]{1,0:T(8,128)(2,1)}), bf16[720,1536]{1,0:T(8,128)(2,1)}) %all-reduce.5.cloned.1.call-update) | async-done | bytes 2211856 | tf_op jit(solution)/shard_map/psum | solution.py:77
  428.5 5.2 %add_convert_fusion = bf16[720,1536]{1,0:T(8,128)(2,1)} fusion(bf16[720,1536]{1,0:T(8,128)(2,1)} %all-reduce.5.cloned.1.call-done, bf16[720,1536]{1,0:T(8,128)(2,1)} %all-reduce.3.cloned.1.call-done, bf16[720,1536]{1,0:T(8,128)(2,1)} %param.9), kind=kLoop, calls=%fused_computation.23 | loop fusion | flops 6635520 | bytes 8847360 | tf_op jit(solution)/shard_map/convert_element_type | solution.py:77
  (128 shorter events, 71.5 us)
Async XLA Ops:
  6.5 329.9 %copy-start = (bf16[768,1536]{1,0:T(8,128)(2,1)S(1)}, bf16[768,1536]{1,0:T(8,128)(2,1)}, u32[]{:S(2)}) copy-start(bf16[768,1536]{1,0:T(8,128)(2,1)} %param.15) | copy-start | bytes 7077892
  6.5 4.6 %copy-start.5 = (f32[1536]{0:T(1024)S(1)}, f32[1536]{0:T(1024)}, u32[]{:S(2)}) copy-start(f32[1536]{0:T(1024)} %param.10) | copy-start | bytes 18436
  6.5 68.1 %all-gather.7.cloned.1.call-start = ((), (), s32[]{:S(2)}) async-start(), calls=%async_computation.3 | async-start | bytes 5013504 | tf_op jit(solution)/shard_map/all_gather | solution.py:55
  6.5 4.6 %copy-start.1 = (bf16[720,1536]{1,0:T(8,128)(2,1)S(1)}, bf16[720,1536]{1,0:T(8,128)(2,1)}, u32[]{:S(2)}) copy-start(bf16[720,1536]{1,0:T(8,128)(2,1)} %param.9) | copy-start | bytes 6635524
  6.5 4.6 %copy-start.4 = (bf16[1536,3,192]{0,2,1:T(8,128)(2,1)S(1)}, bf16[1536,3,192]{0,2,1:T(8,128)(2,1)}, u32[]{:S(2)}) copy-start(bf16[1536,3,192]{0,2,1:T(8,128)(2,1)} %param.11) | copy-start | bytes 5308420
  13.8 120.0 %all-gather.5.cloned.1.call-start = ((), (), s32[]{:S(2)}) async-start(), calls=%async_computation.2 | async-start | bytes 5013504 | tf_op jit(solution)/shard_map/all_gather | solution.py:54
  14.5 317.3 %all-reduce.3.cloned.1.call-start = ((), (), s32[]{:S(2)}) async-start(), calls=%async_computation | async-start | bytes 4423680 | tf_op jit(solution)/shard_map/psum | solution.py:71
  250.5 86.0 %copy-start.6 = (f32[1536]{0:T(1024)S(1)}, f32[1536]{0:T(1024)}, u32[]{:S(2)}) copy-start(f32[1536]{0:T(1024)} %param.13) | copy-start | bytes 18436
  250.5 178.0 %all-reduce.5.cloned.1.call-start = ((), (), s32[]{:S(2)}) async-start(), calls=%async_computation.1 | async-start | bytes 4423680 | tf_op jit(solution)/shard_map/psum | solution.py:77
  331.9 3.1 copy-start.2
  331.9 3.6 copy-start.3
Sparse Core Ops, SparseCore 0:
  13.9 60.6 all-gather.6
  77.0 56.7 all-gather.4
  250.6 81.2 all-reduce.2
  345.5 82.9 all-reduce.4
where the time goes:
time: 441 us; the launch traced here: 440 us
  waiting for transfers between devices  267 us (61%)
  matrix products  62.9 us (14%)
  local copies, waits for them, and re-layouts  57.6 us (13%)
  other arithmetic  38.5 us (9%)
  between operations  13.3 us (3%)
    psum x1, waiting for transfers between devices, per_device(): lax.psum(mlp_term.astype(jnp.bfloat16), 'tensor').astype(jnp.float32)  83.1 us
    psum x1, waiting for transfers between devices, per_device(): lax.psum(attn_term.astype(jnp.bfloat16), 'tensor').astype(jnp.float32)  81.1 us
    all_gather x1, waiting for transfers between devices, per_device(): value_piece = lax.all_gather(value, 'seq', axis=0, tiled=True)  60 us
    all_gather x1, waiting for transfers between devices, per_device(): key_piece = lax.all_gather(key, 'seq', axis=0, tiled=True)  41.7 us
    dot_general x16, matrix products, attend_block(): jnp.einsum('hqk,khd->hqd', weights.astype(jnp.bfloat16), values, preferre...  27.2 us
    reduce_sum x16, other arithmetic, attend_block(): total = total * factor + jnp.sum(weights, axis=-1)  24.1 us
    dot_general x16, matrix products, attend_block(): jnp.einsum('qhd,khd->hqk', queries, keys, preferred_element_type=jnp.floa...  21.9 us
    unnamed x17, local copies, waits for them, and re-layouts  21.9 us
  transfers between devices with their start and end apart: 4, of which 4 were waited for; matrix products, arithmetic and copies ran while one was open for 4% of the time, Pallas kernels for 0%

commit v1 on v0

v1 whole, which is shorter than its diff:
```python
import functools

import jax
import jax.numpy as jnp
from jax import lax
from jax.experimental import pallas as pl
from jax.experimental.pallas import tpu as pltpu
from jax.sharding import PartitionSpec as P

HD = 48
ROWS = 720
PAD = 768
NSEQ = 16
NTEN = 8
W = 256
NC = PAD // W
f32 = jnp.float32
bf16 = jnp.bfloat16
MESH = pl.DeviceIdType.MESH

OWN, A, B, C, F, D, E, G = range(8)
DZ = (0, 0, 0, 1, 0, 1, 1, 1)
DY = (0, 3, 1, 0, 2, 3, 1, 2)
ORDER = (
    (OWN, 0), (OWN, 1), (A, 0), (B, 0), (C, 0), (A, 1), (B, 1), (C, 1),
    (F, 0), (F, 1), (D, 0), (E, 0), (D, 1), (E, 1), (G, 0), (G, 1),
)
ARRIVE = {0: ((OWN, 1),), 1: ((A, 0), (B, 0), (C, 0)), 4: ((A, 1),), 5: ((B, 1),), 6: ((C, 1),), 7: ((F, 0),), 8: ((F, 1),),
          9: ((D, 0), (E, 0)), 11: ((D, 1),), 12: ((E, 1),), 13: ((G, 0),), 14: ((G, 1),)}


def layer_norm(values, gain):
    mean = jnp.mean(values, axis=-1, keepdims=True)
    centred = values - mean
    var = jnp.mean(centred * centred, axis=-1, keepdims=True)
    return centred * lax.rsqrt(var + 1e-05) * gain


def attention_kernel(qkv, out, kt, vt, s0, s1, p0, p1, acc, peak, ssem, rsem, tsend, trecv):
    me = lax.axis_index("seq")
    ti = lax.axis_index("tensor")
    zh, yy, core = lax.div(me, 8), lax.rem(lax.div(me, 2), 4), lax.rem(me, 2)
    zl, xx = lax.div(ti, 4), lax.rem(ti, 4)

    def seq_id(off, other=0):
        return (lax.rem(zh + DZ[off], 2) * 4 + lax.rem(yy + DY[off], 4)) * 2 + lax.rem(core + other, 2)

    def ten_id(dz, dx):
        return lax.rem(zl + dz, 2) * 4 + lax.rem(xx + dx, 4)

    seq_near = [seq_id(OWN, 1), seq_id(A), seq_id(B), seq_id(C)]
    ten_near = [ten_id(0, 1), ten_id(0, 3), ten_id(1, 0), ten_id(1, 1), ten_id(1, 3)]
    barrier = pltpu.get_barrier_semaphore()
    for d in seq_near:
        pl.semaphore_signal(barrier, inc=1, device_id={"seq": d}, device_id_type=MESH)
    for d in ten_near:
        pl.semaphore_signal(barrier, inc=1, device_id={"tensor": d}, device_id_type=MESH)

    lane = lax.broadcasted_iota(jnp.int32, (16, PAD), 1)
    row = lax.broadcasted_iota(jnp.int32, (16, PAD), 0)
    ones = jnp.where((row == 0) & (lane < ROWS), 1.0, 0.0).astype(bf16)

    def fill(s, _):
        for h in range(4):
            vt[s, h, HD:64, :] = ones
        return 0

    lax.fori_loop(0, NSEQ, fill, 0)
    for h in range(4):
        kt[me, h] = qkv[1, h]
        vt[me, h, 0:HD, :] = qkv[2, h]
    peak[...] = jnp.full(peak.shape, -1e30, f32)
    acc[...] = jnp.zeros(acc.shape, f32)
    p0[ROWS:PAD, :] = jnp.zeros((PAD - ROWS, PAD), bf16)
    p1[ROWS:PAD, :] = jnp.zeros((PAD - ROWS, PAD), bf16)
    pl.semaphore_wait(barrier, len(seq_near) + len(ten_near))

    sent = [[], []]

    def block_ref(piece, slot, hp):
        ref = kt if piece == 0 else vt
        return ref.at[slot, 2 * hp : 2 * hp + 2, 0:HD]

    def seq_copy(piece, slot, hp, dest, index, own=False):
        src = qkv.at[1 + piece, 2 * hp : 2 * hp + 2] if own else block_ref(piece, slot, hp)
        return pltpu.make_async_remote_copy(
            src_ref=src, dst_ref=block_ref(piece, slot, hp), send_sem=ssem.at[hp, index],
            recv_sem=rsem.at[slot, hp, piece], device_id={"seq": dest}, device_id_type=MESH,
        )

    def send(piece, slot, hp, dest, own=False):
        c = seq_copy(piece, slot, hp, dest, len(sent[hp]), own)
        c.start()
        sent[hp].append(piece)

    def send_own(hp):
        for piece in (0, 1):
            for d in (seq_id(B), seq_id(A), seq_id(C), seq_id(OWN, 1)):
                send(piece, me, hp, d, own=True)

    def arrive(hp, off, other):
        slot = seq_id(off, other)
        for piece in (0, 1):
            seq_copy(piece, slot, hp, me, 0).wait_recv()
        if other:
            return
        if off in (A, D):
            send(0, slot, hp, seq_id(B))
        if off in (B, E):
            send(1, slot, hp, seq_id(A))
        for piece in (0, 1):
            send(piece, slot, hp, seq_id(OWN, 1))

    def spread(hp):
        slot = seq_id(C)
        for piece in (0, 1):
            for d in (seq_id(B), seq_id(A)):
                send(piece, slot, hp, d)

    tsent = []

    def ten_copy(src, head, dest, index):
        return pltpu.make_async_remote_copy(
            src_ref=out.at[src, head], dst_ref=out.at[src, head], send_sem=tsend.at[index],
            recv_sem=trecv.at[src, head], device_id={"tensor": dest}, device_id_type=MESH,
        )

    def ten_start(src, head, dest):
        c = ten_copy(src, head, dest, len(tsent))
        c.start()
        tsent.append(0)

    def finish(hp):
        for h in (2 * hp, 2 * hp + 1):
            out[ti, h] = (acc[h, 0:HD, :] / acc[h, HD : HD + 1, :]).astype(bf16)
        for h in (2 * hp, 2 * hp + 1):
            for d in ten_near:
                ten_start(ti, h, d)

    def ten_wait(src, head):
        ten_copy(src, head, ti, 0).wait_recv()

    def relay(hp):
        for dz in (0, 1):
            left, right = ten_id(dz, 3), ten_id(dz, 1)
            for h in (2 * hp, 2 * hp + 1):
                ten_wait(left, h)
                ten_wait(right, h)
            ten_start(left, 2 * hp, ten_id(0, 1))
            ten_start(right, 2 * hp + 1, ten_id(0, 3))

    def collect(hp):
        for h in (2 * hp, 2 * hp + 1):
            ten_wait(ten_id(1, 0), h)
            ten_wait(ten_id(0, 2), h)
            ten_wait(ten_id(1, 2), h)

    S, Pw = (s0, s1), (p0, p1)

    def slot_at(pos):
        code = pos * 0
        for j, (off, other) in enumerate(ORDER):
            code = code + (pos == j).astype(jnp.int32) * (DZ[off] * 8 + DY[off] * 2 + other)
        dz, dy, dc = lax.div(code, 8), lax.rem(lax.div(code, 2), 4), lax.rem(code, 2)
        return (lax.rem(zh + dz, 2) * 4 + lax.rem(yy + dy, 4)) * 2 + lax.rem(core + dc, 2)

    def score_pieces(slot, head, par, top):
        def mk(c, half):
            cs = slice(c * W, (c + 1) * W)

            def go():
                lo = half * 384
                n = 384 if half == 0 else ROWS - 384
                s = lax.dot_general(
                    kt[slot, head, :, lo : lo + 384], qkv[0, head, :, cs], (((0,), (0,)), ((), ())), preferred_element_type=f32
                )[0:n]
                S[par][lo : lo + n, cs] = s
                b = jnp.max(s.reshape(-1, 8, W), axis=0)
                top[c] = b if c not in top else jnp.maximum(top[c], b)

            return go

        return [mk(c, half) for c in range(NC) for half in (0, 1)]

    def weight_pieces(par, now):
        def mk(c, r):
            cs = slice(c * W, (c + 1) * W)

            def go():
                Pw[par][r : r + 240, cs] = jnp.exp2(S[par][r : r + 240, cs] - now[c]).astype(bf16)

            return go

        return [mk(c, r) for c in range(NC) for r in (0, 240, 480)]

    def value_pieces(slot, head, par, factor):
        def mk(c):
            cs = slice(c * W, (c + 1) * W)

            def go():
                acc[head, :, cs] = acc[head, :, cs] * factor[c] + jnp.dot(
                    vt[slot, head], Pw[par][:, cs], preferred_element_type=f32
                )

            return go

        return [mk(c) for c in range(NC)]

    def interleave(*lists):
        events = []
        for k, items in enumerate(lists):
            for j, x in enumerate(items):
                events.append(((j + 0.5) / len(items), k, x))
        events.sort(key=lambda e: (e[0], e[1]))
        for _, _, x in events:
            x()

    def keep_top(head, top):
        for c in range(NC):
            peak[head, 8:16, c * W : (c + 1) * W] = top[c]

    def step(t, _):
        for hp in (0, 1):
            for j, blocks in ARRIVE.items():

                @pl.when(t == 16 * hp + j)
                def _(hp=hp, j=j, blocks=blocks):
                    for off, other in blocks:
                        arrive(hp, off, other)
                    if j == 1:
                        spread(hp)
                    if j == 9 and hp == 0:
                        send_own(1)

        @pl.when(t == 16)
        def _():
            finish(0)

        @pl.when(t == 22)
        def _():
            relay(0)

        @pl.when(t == 28)
        def _():
            collect(0)

        hp = lax.div(t, 16)
        slot = slot_at(lax.rem(t, 16))
        nxt = lax.rem(t + 1, 32)
        slot_next = slot_at(lax.rem(nxt, 16))
        held = None
        for k in (0, 1):
            head = 2 * hp + k
            now, factor = {}, {}
            for c in range(NC):
                cs = slice(c * W, (c + 1) * W)
                old = peak[head, 0:1, cs]
                now[c] = jnp.maximum(old, jnp.max(peak[head, 8:16, cs], axis=0, keepdims=True))
                factor[c] = jnp.exp2(old - now[c])
                peak[head, 0:1, cs] = now[c]
            head_n = head + 1 if k == 0 else 2 * lax.div(nxt, 16)
            slot_n = slot if k == 0 else slot_next
            top = {}
            scores = score_pieces(slot_n, head_n, 1 - k, top)
            weights = weight_pieces(k, now)
            if held is None:
                interleave(scores, weights)
                held = value_pieces(slot, head, k, factor)
            else:
                interleave(scores, weights, held)
                for x in value_pieces(slot, head, k, factor):
                    x()
            keep_top(head_n, top)
        return 0

    send_own(0)
    top = {}
    for x in score_pieces(me, 0, 0, top):
        x()
    keep_top(0, top)
    lax.fori_loop(0, 32, step, 0)
    finish(1)
    relay(1)
    collect(1)
    for hp in (0, 1):
        for index, piece in enumerate(sent[hp]):
            seq_copy(piece, me, hp, me, index).wait_send()
    for index in range(len(tsent)):
        ten_copy(ti, 0, ti, index).wait_send()


def attention(qkv):
    vmem = pl.BlockSpec(memory_space=pltpu.VMEM)
    return pl.pallas_call(
        attention_kernel,
        out_shape=jax.ShapeDtypeStruct((NTEN, 4, HD, PAD), bf16),
        in_specs=[vmem],
        out_specs=vmem,
        scratch_shapes=[
            pltpu.VMEM((NSEQ, 4, HD, PAD), bf16),
            pltpu.VMEM((NSEQ, 4, 64, PAD), bf16),
            pltpu.VMEM((ROWS, PAD), f32),
            pltpu.VMEM((ROWS, PAD), f32),
            pltpu.VMEM((PAD, PAD), bf16),
            pltpu.VMEM((PAD, PAD), bf16),
            pltpu.VMEM((4, 64, PAD), f32),
            pltpu.VMEM((4, 16, PAD), f32),
            pltpu.SemaphoreType.DMA((2, 32)),
            pltpu.SemaphoreType.DMA((NSEQ, 2, 2)),
            pltpu.SemaphoreType.DMA((32,)),
            pltpu.SemaphoreType.DMA((NTEN, 4)),
        ],
        compiler_params=pltpu.CompilerParams(collective_id=0, has_side_effects=True, vmem_limit_bytes=48 * 2**20),
        cost_estimate=pl.CostEstimate(flops=60_000_000_000, bytes_accessed=4_000_000, transcendentals=33_000_000),
        name="attention",
    )(qkv)


def per_device(tokens, norm_gain, w_qkv, w_out, post_gain, w_up, w_down):
    w_full = lax.all_gather(w_out, "tensor", axis=0, tiled=True)
    base = tokens.astype(f32)
    normed = layer_norm(base, norm_gain).astype(bf16)
    qkv = lax.dot_general(w_qkv.reshape(w_qkv.shape[0], -1), normed, (((0,), (1,)), ((), ())), preferred_element_type=f32)
    scale = jnp.concatenate([jnp.full((192, 1), 1.4426950408889634 / HD**0.5, f32), jnp.ones((384, 1), f32)])
    qkv = jnp.pad((qkv * scale).astype(bf16), ((0, 0), (0, PAD - ROWS))).reshape(3, 4, HD, PAD)
    attended = attention(qkv).reshape(NTEN * 4 * HD, PAD)
    mixed = base + lax.dot_general(attended, w_full, (((0,), (0,)), ((), ())), preferred_element_type=f32)[:ROWS]
    post = layer_norm(mixed, post_gain).astype(bf16)
    hidden = jax.nn.gelu(jnp.dot(post, w_up, preferred_element_type=f32), approximate=True).astype(bf16)
    mlp_term = jnp.dot(hidden, w_down, preferred_element_type=f32)
    return (mixed + lax.psum(mlp_term.astype(bf16), "tensor").astype(f32)).astype(bf16)


def solution(mesh):
    placed = (P("seq", None), P(), P(None, None, "tensor"), P("tensor", None), P(), P(None, "tensor"), P("tensor", None))
    return jax.shard_map(per_device, mesh=mesh, in_specs=placed, out_specs=P("seq", None), check_vma=False)
```

time: 441 us -> 260 us (0.59)
  waiting for transfers between devices: 267 us -> 83.2 us
  Pallas kernels: 0 us -> 132 us
  local copies, waits for them, and re-layouts: 57.6 us -> 3.66 us
  matrix products: 62.9 us -> 18.1 us
  other arithmetic: 38.5 us -> 8.43 us
    pallas_call x0 -> x1, Pallas kernels: none -> 132 us  [attention(): pl.pallas_call(attention_kernel, out_shape=jax.ShapeDtypeStruct((NTEN, 4,...]
    all_gather x2 -> x1, waiting for transfers between devices: 102 us -> 0.01 us  [per_device(): w_full = lax.all_gather(w_out, 'tensor', axis=0, tiled=True)]
    psum x2 -> x1, waiting for transfers between devices: 164 us -> 82.5 us  [per_device(): lax.psum(mlp_term.astype(bf16), 'tensor').astype(f32)]
    dot_general x35 -> x3, matrix products: 62.9 us -> 18.1 us  [the longest x1 8.91 us: per_device(): mlp_term = jnp.dot(hidden, w_down, preferred_element_type=f32)]
    reduce_sum x16 -> x0, other arithmetic: 24.1 us -> none  [attend_block(): total = total * factor + jnp.sum(weights, axis=-1)]
    dynamic_slice x16 -> x0, local copies, waits for them, and re-layouts: 21.3 us -> none  [step(): value_block = lax.dynamic_slice_in_dim(value_piece, first, block, 0)]
    unnamed x17 -> x16, local copies, waits for them, and re-layouts: 21.9 us -> 3.58 us
    all_gather x2 -> x0, local copies, waits for them, and re-layouts: 14.3 us -> none  [the longest x1 7.2 us: per_device(): value_piece = lax.all_gather(value, 'seq', axis=0, tiled=True)]
  transfers between devices with their start and end apart: 4 -> 2, of which waited for: 4 -> 1; matrix products, arithmetic and copies ran while one was open for 4% -> 2% of each run, Pallas kernels for 0% -> 51%
where the time goes in v1:
time: 260 us; the launch traced here: 259 us
  Pallas kernels  132 us (51%)
  waiting for transfers between devices  83.2 us (32%)
  matrix products  18.1 us (7%)
  between operations  13.6 us (5%)
  other arithmetic  8.43 us (3%)
  local copies, waits for them, and re-layouts  3.66 us (1%)
    pallas_call x1, Pallas kernels, attention(): pl.pallas_call(attention_kernel, out_shape=jax.ShapeDtypeStruct((NTEN, 4,...  132 us
    psum x1, waiting for transfers between devices, per_device(): lax.psum(mlp_term.astype(bf16), 'tensor').astype(f32)  82.5 us
    dot_general x1, matrix products, per_device(): mlp_term = jnp.dot(hidden, w_down, preferred_element_type=f32)  8.91 us
    dot_general x1, matrix products, per_device(): lax.dot_general(attended, w_full, (((0,), (0,)), ((), ())), preferred_ele...  7.54 us
  transfers between devices with their start and end apart: 2, of which 1 were waited for; matrix products, arithmetic and copies ran while one was open for 2% of the time, Pallas kernels for 51%

profile of v1, /device:TPU:0, one launch (start us, length us, event | category | flops | bytes accessed | tf_op | source)
XLA Modules:
  0.0 259.4 jit_solution(7787135100395410244)
XLA Ops:
  6.5 0.0 copy-start
  6.5 0.0 all-gather.2.cloned.1.call-start
  6.5 0.7 all-gather.2.cloned.1.call-update
  7.3 0.0 copy-start.5
  7.3 0.0 copy-start.7
  7.3 0.0 all-reduce.3.cloned.1.call-start
  7.3 0.0 copy-start.3
  7.3 0.0 copy-start.4
  7.3 2.1 convert_reduce_fusion
  9.5 0.1 copy-done.3
  9.6 0.7 fusion.2
  10.3 0.0 copy-done.5
  10.4 0.0 copy-done.7
  10.4 0.0 copy-done.4
  10.4 1.7 fusion.25
  12.1 0.1 pad.4
  12.2 132.4 %attention.1 = bf16[8,4,48,768]{3,2,1,0:T(8,128)(2,1)S(1)} custom-call(bf16[3,4,48,768]{3,2,1,0:T(8,128)(2,1)S(1)} %bitcast.9), custom_call_target="tpu_custom_call" | custom-call | flops 60000002048 | bytes 4000000 | tf_op jit(solution)/shard_map/attention/pallas_call | solution.py:294
  144.6 0.0 copy-start.1
  144.6 1.4 copy-done.1
  146.0 0.0 all-gather.2.cloned.1.call-done
  146.0 7.5 %fusion.32 = (f32[720]{0:T(1024)S(1)}, f32[720,1536]{1,0:T(8,128)S(1)}) fusion(bf16[1536,1536]{1,0:T(8,128)(2,1)} %all-gather.2.cloned.1.call-done, bf16[1536,768]{1,0:T(8,128)(2,1)} %bitcast.10, bf16[720,1536]{1,0:T(8,128)(2,1)} %param.7), kind=kOutput, calls=%fused_computation.40 | convolution fusion | flops 3400703232 | bytes 13716288 | tf_op jit(solution)/shard_map/dot_general | solution.py:327
  153.5 0.0 copy-start.2
  153.6 0.0 copy-start.6
  153.6 2.0 copy-done.2
  155.6 0.6 multiply_reduce_fusion
  156.2 0.0 copy-done
  156.2 0.0 copy-done.6
  156.2 8.9 %convolution_convert_fusion = bf16[720,1536]{1,0:T(8,128)(2,1)} fusion(bf16[768,1536]{1,0:T(8,128)(2,1)S(1)} %copy-done, bf16[1536,768]{1,0:T(8,128)(2,1)} %param.12, f32[720,1536]{1,0:T(8,128)} %copy-done.2, f32[1536]{0:T(1024)S(1)} %copy-done.6, f32[720]{0:T(1024)S(1)} %add_rsqrt_fusion, f32[720]{0:T(1024)S(1)} %broadcast_multiply_fusion), kind=kOutput, calls=%fused_computation.12 | convolution fusion | flops 3407892480 | bytes 11366016 | tf_op jit(solution)/shard_map/dot_general | solution.py:330
  165.1 0.0 all-reduce.3.cloned.1.call-update
  165.1 82.5 %all-reduce.3.cloned.1.call-done = bf16[720,1536]{1,0:T(8,128)(2,1)} async-done(((bf16[720,1536]{1,0:T(8,128)(2,1)}), bf16[720,1536]{1,0:T(8,128)(2,1)}) %all-reduce.3.cloned.1.call-update) | async-done | bytes 2211856 | tf_op jit(solution)/shard_map/psum | solution.py:331
  247.6 5.0 %add_convert_fusion = bf16[720,1536]{1,0:T(8,128)(2,1)} fusion(f32[720,1536]{1,0:T(8,128)} %copy-done.2, bf16[720,1536]{1,0:T(8,128)(2,1)} %all-reduce.3.cloned.1.call-done), kind=kLoop, calls=%fused_computation.8 | loop fusion | flops 3317760 | bytes 8847360 | tf_op jit(solution)/shard_map/convert_element_type | solution.py:331
  (4 shorter events, 0.0 us)
Async XLA Ops:
  6.5 149.6 %copy-start = (bf16[768,1536]{1,0:T(8,128)(2,1)S(1)}, bf16[768,1536]{1,0:T(8,128)(2,1)}, u32[]{:S(2)}) copy-start(bf16[768,1536]{1,0:T(8,128)(2,1)} %param.13) | copy-start | bytes 7077892
  6.5 139.5 %all-gather.2.cloned.1.call-start = ((), (), s32[]{:S(2)}) async-start(), calls=%async_computation | async-start | bytes 5308416 | tf_op jit(solution)/shard_map/all_gather | solution.py:320
  7.3 3.1 %copy-start.5 = (f32[1536]{0:T(1024)S(1)}, f32[1536]{0:T(1024)}, u32[]{:S(2)}) copy-start(f32[1536]{0:T(1024)} %param.8) | copy-start | bytes 18436
  7.3 3.1 %copy-start.7 = (f32[576]{0:T(1024)S(1)}, f32[576]{0:T(1024)}, u32[]{:S(2)}) copy-start(f32[576]{0:T(1024)} %constant.18.clone.1) | copy-start | bytes 6916
  7.3 240.3 %all-reduce.3.cloned.1.call-start = ((), (), s32[]{:S(2)}) async-start(), calls=%async_computation.1 | async-start | bytes 4423680 | tf_op jit(solution)/shard_map/psum | solution.py:331
  7.3 2.3 copy-start.3
  7.3 3.0 %copy-start.4 = (bf16[1536,3,192]{0,2,1:T(8,128)(2,1)S(1)}, bf16[1536,3,192]{0,2,1:T(8,128)(2,1)}, u32[]{:S(2)}) copy-start(bf16[1536,3,192]{0,2,1:T(8,128)(2,1)} %param.9) | copy-start | bytes 5308420
  144.6 1.4 copy-start.1
  153.5 2.0 copy-start.2
  153.6 2.6 %copy-start.6 = (f32[1536]{0:T(1024)S(1)}, f32[1536]{0:T(1024)}, u32[]{:S(2)}) copy-start(f32[1536]{0:T(1024)} %param.11) | copy-start | bytes 18436
Sparse Core Ops, SparseCore 0:
  9.0 64.0 all-gather.1
  165.2 82.3 all-reduce.2

commit v2 on v1

--- a/solution.py
+++ b/solution.py
@@ -36,7 +36,9 @@
     return centred * lax.rsqrt(var + 1e-05) * gain
 
 
-def attention_kernel(qkv, out, kt, vt, s0, s1, p0, p1, acc, peak, ssem, rsem, tsend, trecv):
+def layer_kernel(qkv, gain, tokens, w_out, w_up, w_down, out, kt, vt, s0, s1, p0, p1, acc, peak, att, wf, tok, wu, wd,
+                 mixed, post, term, ra, rb, ra2, rb2, sa2, sb2, ssem, rsem, tsend, trecv, wsend, wrecv, lsem,
+                 qsend, rarecv, rbrecv, ra2recv, rb2recv, gsend, grecv):
     me = lax.axis_index("seq")
     ti = lax.axis_index("tensor")
     zh, yy, core = lax.div(me, 8), lax.rem(lax.div(me, 2), 4), lax.rem(me, 2)
@@ -50,10 +52,20 @@
 
     seq_near = [seq_id(OWN, 1), seq_id(A), seq_id(B), seq_id(C)]
     ten_near = [ten_id(0, 1), ten_id(0, 3), ten_id(1, 0), ten_id(1, 1), ten_id(1, 3)]
+    ten_all = [ten_id(0, 1), ten_id(0, 3), ten_id(0, 2), ten_id(1, 0), ten_id(1, 1), ten_id(1, 3)]
+    own_rows = pl.ds(pl.multiple_of(ti * 192, 16), 192)
+    loads = [
+        pltpu.make_async_copy(w_out, wf.at[own_rows], lsem.at[0]),
+        pltpu.make_async_copy(w_up, wu, lsem.at[1]),
+        pltpu.make_async_copy(w_down, wd, lsem.at[2]),
+        pltpu.make_async_copy(tokens, tok.at[0:ROWS], lsem.at[3]),
+    ]
+    for c in loads:
+        c.start()
     barrier = pltpu.get_barrier_semaphore()
     for d in seq_near:
         pl.semaphore_signal(barrier, inc=1, device_id={"seq": d}, device_id_type=MESH)
-    for d in ten_near:
+    for d in ten_all:
         pl.semaphore_signal(barrier, inc=1, device_id={"tensor": d}, device_id_type=MESH)
 
     lane = lax.broadcasted_iota(jnp.int32, (16, PAD), 1)
@@ -73,7 +85,8 @@
     acc[...] = jnp.zeros(acc.shape, f32)
     p0[ROWS:PAD, :] = jnp.zeros((PAD - ROWS, PAD), bf16)
     p1[ROWS:PAD, :] = jnp.zeros((PAD - ROWS, PAD), bf16)
-    pl.semaphore_wait(barrier, len(seq_near) + len(ten_near))
+    tok[ROWS:PAD, :] = jnp.zeros((PAD - ROWS, 1536), bf16)
+    pl.semaphore_wait(barrier, len(seq_near) + len(ten_all))
 
     sent = [[], []]
 
@@ -119,9 +132,12 @@
 
     tsent = []
 
+    def head_ref(src, head):
+        return att.at[pl.ds(pl.multiple_of(src * 192 + head * HD, 16), HD)]
+
     def ten_copy(src, head, dest, index):
         return pltpu.make_async_remote_copy(
-            src_ref=out.at[src, head], dst_ref=out.at[src, head], send_sem=tsend.at[index],
+            src_ref=head_ref(src, head), dst_ref=head_ref(src, head), send_sem=tsend.at[index],
             recv_sem=trecv.at[src, head], device_id={"tensor": dest}, device_id_type=MESH,
         )
 
@@ -132,7 +148,7 @@
 
     def finish(hp):
         for h in (2 * hp, 2 * hp + 1):
-            out[ti, h] = (acc[h, 0:HD, :] / acc[h, HD : HD + 1, :]).astype(bf16)
+            att[pl.ds(pl.multiple_of(ti * 192 + h * HD, 16), HD), :] = (acc[h, 0:HD, :] / acc[h, HD : HD + 1, :]).astype(bf16)
         for h in (2 * hp, 2 * hp + 1):
             for d in ten_near:
                 ten_start(ti, h, d)
@@ -154,6 +170,69 @@
             ten_wait(ten_id(1, 0), h)
             ten_wait(ten_id(0, 2), h)
             ten_wait(ten_id(1, 2), h)
+
+    wsent = []
+
+    def w_copy(src, half, other, dest, index):
+        at = lax.rem(core + other, 2)
+        ref = wf.at[pl.ds(pl.multiple_of(src * 192 + at * 96 + half * 48, 16), 48)]
+        return pltpu.make_async_remote_copy(
+            src_ref=ref, dst_ref=ref, send_sem=wsend.at[index], recv_sem=wrecv.at[src, other, half],
+            device_id=dest, device_id_type=MESH,
+        )
+
+    def w_start(src, half, dest, index_other=0):
+        at = core
+        ref = wf.at[pl.ds(pl.multiple_of(src * 192 + at * 96 + half * 48, 16), 48)]
+        pltpu.make_async_remote_copy(
+            src_ref=ref, dst_ref=ref, send_sem=wsend.at[len(wsent)], recv_sem=wrecv.at[src, index_other, half],
+            device_id=dest, device_id_type=MESH,
+        ).start()
+        wsent.append(0)
+
+    def w_wait(src, half, other):
+        w_copy(src, half, other, {"tensor": ti}, 0).wait_recv()
+
+    def w_share(src):
+        for half in (0, 1):
+            w_start(src, half, {"seq": seq_id(OWN, 1)}, 1)
+
+    def w_own():
+        loads[0].wait()
+        for half in (0, 1):
+            for d in (ten_id(0, 1), ten_id(0, 3), ten_id(1, 0)):
+                w_start(ti, half, {"tensor": d})
+
+    def w_relay(dz):
+        left, right = ten_id(dz, 3), ten_id(dz, 1)
+        for src in (left, right):
+            for half in (0, 1):
+                w_wait(src, half, 0)
+        w_start(left, 0, {"tensor": ten_id(0, 1)})
+        w_start(right, 1, {"tensor": ten_id(0, 3)})
+        w_share(left)
+        w_share(right)
+
+    def w_cross():
+        src = ten_id(1, 0)
+        for half in (0, 1):
+            w_wait(src, half, 0)
+            for d in (ten_id(0, 1), ten_id(0, 3)):
+                w_start(src, half, {"tensor": d})
+        w_share(src)
+
+    def w_far(dz):
+        src = ten_id(dz, 2)
+        for half in (0, 1):
+            w_wait(src, half, 0)
+        w_share(src)
+
+    def w_collect():
+        for dz in (0, 1):
+            for dx in range(4):
+                if (dz, dx) != (0, 0):
+                    for half in (0, 1):
+                        w_wait(ten_id(dz, dx), half, 1)
 
     S, Pw = (s0, s1), (p0, p1)
 
@@ -232,6 +311,20 @@
                     if j == 9 and hp == 0:
                         send_own(1)
 
+        @pl.when(t == 5)
+        def _():
+            w_cross()
+            w_relay(0)
+
+        @pl.when(t == 12)
+        def _():
+            w_relay(1)
+            w_far(0)
+
+        @pl.when(t == 15)
+        def _():
+            w_far(1)
+
         @pl.when(t == 16)
         def _():
             finish(0)
@@ -243,6 +336,7 @@
         @pl.when(t == 28)
         def _():
             collect(0)
+            w_collect()
 
         hp = lax.div(t, 16)
         slot = slot_at(lax.rem(t, 16))
@@ -274,6 +368,7 @@
         return 0
 
     send_own(0)
+    w_own()
     top = {}
     for x in score_pieces(me, 0, 0, top):
         x()
@@ -282,19 +377,133 @@
     finish(1)
     relay(1)
     collect(1)
+    for c in loads[1:]:
+        c.wait()
+
+    def project(c, _):
+        cols = pl.ds(pl.multiple_of(c * W, W), W)
+        m = tok[cols, :].astype(f32) + lax.dot_general(
+            att[:, cols], wf[...], (((0,), (0,)), ((), ())), preferred_element_type=f32
+        )
+        mixed[cols, :] = m
+        post[cols, :] = layer_norm(m, gain[...]).astype(bf16)
+        return 0
+
+    lax.fori_loop(0, NC, project, 0)
+
+    def rows_of(t, half=0, n=48):
+        return pl.ds(pl.multiple_of(t * 96 + half * 48, 16), n)
+
+    qsent = []
+
+    def q_copy(src_ref, dst_ref, recv, dest, index):
+        return pltpu.make_async_remote_copy(
+            src_ref=src_ref, dst_ref=dst_ref, send_sem=qsend.at[index], recv_sem=recv,
+            device_id={"tensor": dest}, device_id_type=MESH,
+        )
+
+    def q_start(src_ref, dst_ref, recv, dest):
+        q_copy(src_ref, dst_ref, recv, dest, len(qsent)).start()
+        qsent.append(0)
+
+    def q_wait(ref, recv):
+        q_copy(ref, ref, recv, ti, 0).wait_recv()
+
+    def part(t, half):
+        return term[rows_of(t, half), :].astype(f32)
+
+    for dx in (2, 1, 3, 0):
+        t0, t1 = ten_id(0, dx), ten_id(1, dx)
+        both = jnp.concatenate([post[rows_of(t0, 0, 96), :], post[rows_of(t1, 0, 96), :]], axis=0)
+        u = jnp.dot(both, wu[...], preferred_element_type=f32)
+        h = jax.nn.gelu(u, approximate=True).astype(bf16)
+        y = jnp.dot(h, wd[...], preferred_element_type=f32).astype(bf16)
+        term[rows_of(t0, 0, 96), :] = y[0:96]
+        term[rows_of(t1, 0, 96), :] = y[96:192]
+        q_start(term.at[rows_of(t1, 1)], rb.at[dx], rbrecv.at[dx], ten_id(1, 0))
+        if dx:
+            for dz, t in ((1, t1), (0, t0)):
+                q_start(term.at[rows_of(t, 0)], ra.at[dz, 3 - dx], rarecv.at[dz, 3 - dx], t0)
+    for dx in (2, 1, 3):
+        q_wait(rb.at[dx], rbrecv.at[dx])
+        sb2[dx - 1] = (part(ten_id(0, dx), 1) + rb[dx].astype(f32)).astype(bf16)
+        q_start(sb2.at[dx - 1], rb2.at[3 - dx], rb2recv.at[3 - dx], ten_id(0, dx))
+    total = part(ten_id(1, 0), 0)
+    for k in range(3):
+        q_wait(ra.at[1, k], rarecv.at[1, k])
+        total = total + ra[1, k].astype(f32)
+    sa2[...] = total.astype(bf16)
+    q_start(sa2, ra2, ra2recv.at[0], ten_id(1, 0))
+
+    gsent = []
+
+    def g_copy(t, half, dest, index):
+        ref = out.at[rows_of(t, half)]
+        return pltpu.make_async_remote_copy(
+            src_ref=ref, dst_ref=ref, send_sem=gsend.at[index], recv_sem=grecv.at[t, half],
+            device_id={"tensor": dest}, device_id_type=MESH,
+        )
+
+    def g_start(t, half, dest):
+        g_copy(t, half, dest, len(gsent)).start()
+        gsent.append(0)
+
+    def g_wait(t, half):
+        g_copy(t, half, ti, 0).wait_recv()
+
+    q_wait(rb.at[0], rbrecv.at[0])
+    total = mixed[rows_of(ti, 1), :] + part(ti, 1) + rb[0].astype(f32)
+    for k in range(3):
+        q_wait(rb2.at[k], rb2recv.at[k])
+        total = total + rb2[k].astype(f32)
+    out[rows_of(ti, 1), :] = total.astype(bf16)
+    g_start(ti, 1, ten_id(1, 0))
+    total = mixed[rows_of(ti, 0), :] + part(ti, 0)
+    for k in range(3):
+        q_wait(ra.at[0, k], rarecv.at[0, k])
+        total = total + ra[0, k].astype(f32)
+    q_wait(ra2, ra2recv.at[0])
+    total = total + ra2[...].astype(f32)
+    out[rows_of(ti, 0), :] = total.astype(bf16)
+    for dx in (1, 3, 2):
+        g_start(ti, 0, ten_id(0, dx))
+    g_start(ti, 0, ten_id(1, 0))
+    for dx in (1, 3, 2):
+        g_start(ti, 1, ten_id(0, dx))
+    g_wait(ten_id(1, 0), 1)
+    for dx in (1, 3, 2):
+        g_start(ten_id(1, 0), 1, ten_id(0, dx))
+    for dx in (1, 3, 2):
+        g_wait(ten_id(0, dx), 0)
+        g_start(ten_id(0, dx), 0, ten_id(1, 0))
+    for dx in (1, 3, 2):
+        g_wait(ten_id(0, dx), 1)
+    g_wait(ten_id(1, 0), 0)
+    for dx in (1, 3, 2):
+        g_wait(ten_id(1, dx), 0)
+        g_wait(ten_id(1, dx), 1)
+
     for hp in (0, 1):
         for index, piece in enumerate(sent[hp]):
             seq_copy(piece, me, hp, me, index).wait_send()
     for index in range(len(tsent)):
         ten_copy(ti, 0, ti, index).wait_send()
-
-
-def attention(qkv):
+    for index in range(len(wsent)):
+        w_copy(ti, 0, 0, {"tensor": ti}, index).wait_send()
+    for index in range(len(qsent)):
+        q_copy(sa2, ra2, ra2recv.at[0], ti, index).wait_send()
+    for index in range(len(gsent)):
+        g_copy(ti, 0, ti, index).wait_send()
+
+
+def layer(qkv, gain, tokens, w_out, w_up, w_down):
     vmem = pl.BlockSpec(memory_space=pltpu.VMEM)
+    hbm = pl.BlockSpec(memory_space=pl.ANY)
+    D = tokens.shape[1]
     return pl.pallas_call(
-        attention_kernel,
-        out_shape=jax.ShapeDtypeStruct((NTEN, 4, HD, PAD), bf16),
-        in_specs=[vmem],
+        layer_kernel,
+        out_shape=jax.ShapeDtypeStruct((PAD, D), bf16),
+        in_specs=[vmem, vmem, hbm, hbm, hbm, hbm],
         out_specs=vmem,
         scratch_shapes=[
             pltpu.VMEM((NSEQ, 4, HD, PAD), bf16),
@@ -305,30 +514,48 @@
             pltpu.VMEM((PAD, PAD), bf16),
             pltpu.VMEM((4, 64, PAD), f32),
             pltpu.VMEM((4, 16, PAD), f32),
+            pltpu.VMEM((D, PAD), bf16),
+            pltpu.VMEM((D, D), bf16),
+            pltpu.VMEM((PAD, D), bf16),
+            pltpu.VMEM((D, 768), bf16),
+            pltpu.VMEM((768, D), bf16),
+            pltpu.VMEM((PAD, D), f32),
+            pltpu.VMEM((PAD, D), bf16),
+            pltpu.VMEM((PAD, D), bf16),
+            pltpu.VMEM((2, 3, 48, D), bf16),
+            pltpu.VMEM((4, 48, D), bf16),
+            pltpu.VMEM((48, D), bf16),
+            pltpu.VMEM((3, 48, D), bf16),
+            pltpu.VMEM((48, D), bf16),
+            pltpu.VMEM((3, 48, D), bf16),
             pltpu.SemaphoreType.DMA((2, 32)),
             pltpu.SemaphoreType.DMA((NSEQ, 2, 2)),
             pltpu.SemaphoreType.DMA((32,)),
             pltpu.SemaphoreType.DMA((NTEN, 4)),
+            pltpu.SemaphoreType.DMA((32,)),
+            pltpu.SemaphoreType.DMA((NTEN, 2, 2)),
+            pltpu.SemaphoreType.DMA((4,)),
+            pltpu.SemaphoreType.DMA((16,)),
+            pltpu.SemaphoreType.DMA((2, 3)),
+            pltpu.SemaphoreType.DMA((4,)),
+            pltpu.SemaphoreType.DMA((1,)),
+            pltpu.SemaphoreType.DMA((3,)),
+            pltpu.SemaphoreType.DMA((16,)),
+            pltpu.SemaphoreType.DMA((NTEN, 2)),
         ],
-        compiler_params=pltpu.CompilerParams(collective_id=0, has_side_effects=True, vmem_limit_bytes=48 * 2**20),
+        compiler_params=pltpu.CompilerParams(collective_id=0, has_side_effects=True, vmem_limit_bytes=60 * 2**20),
         cost_estimate=pl.CostEstimate(flops=60_000_000_000, bytes_accessed=4_000_000, transcendentals=33_000_000),
-        name="attention",
-    )(qkv)
+        name="layer",
+    )(qkv, gain, tokens, w_out, w_up, w_down)
 
 
 def per_device(tokens, norm_gain, w_qkv, w_out, post_gain, w_up, w_down):
-    w_full = lax.all_gather(w_out, "tensor", axis=0, tiled=True)
     base = tokens.astype(f32)
     normed = layer_norm(base, norm_gain).astype(bf16)
     qkv = lax.dot_general(w_qkv.reshape(w_qkv.shape[0], -1), normed, (((0,), (1,)), ((), ())), preferred_element_type=f32)
     scale = jnp.concatenate([jnp.full((192, 1), 1.4426950408889634 / HD**0.5, f32), jnp.ones((384, 1), f32)])
     qkv = jnp.pad((qkv * scale).astype(bf16), ((0, 0), (0, PAD - ROWS))).reshape(3, 4, HD, PAD)
-    attended = attention(qkv).reshape(NTEN * 4 * HD, PAD)
-    mixed = base + lax.dot_general(attended, w_full, (((0,), (0,)), ((), ())), preferred_element_type=f32)[:ROWS]
-    post = layer_norm(mixed, post_gain).astype(bf16)
-    hidden = jax.nn.gelu(jnp.dot(post, w_up, preferred_element_type=f32), approximate=True).astype(bf16)
-    mlp_term = jnp.dot(hidden, w_down, preferred_element_type=f32)
-    return (mixed + lax.psum(mlp_term.astype(bf16), "tensor").astype(f32)).astype(bf16)
+    return layer(qkv, post_gain[None, :], tokens, w_out, w_up, w_down)[:ROWS]
 
 
 def solution(mesh):

time: 260 us -> 152 us (0.58)
  waiting for transfers between devices: 83.2 us -> 0 us
  matrix products: 18.1 us -> 1.67 us
  between operations: 13.6 us -> 0.06 us
  Pallas kernels: 132 us -> 141 us
  other arithmetic: 8.43 us -> 2.71 us
  local copies, waits for them, and re-layouts: 3.66 us -> 6.88 us
    psum x1 -> x0, waiting for transfers between devices: 82.5 us -> none  [per_device(): lax.psum(mlp_term.astype(bf16), 'tensor').astype(f32)]
    dot_general x2 -> x0, matrix products: 16.4 us -> none  [the longest x1 8.91 us: per_device(): mlp_term = jnp.dot(hidden, w_down, preferred_element_type=f32)]
    pallas_call x1, Pallas kernels: 132 us -> 141 us  [layer(): pl.pallas_call(layer_kernel, out_shape=jax.ShapeDtypeStruct((PAD, D), bf1...]
    convert_element_type x1 -> x0, other arithmetic: 5.01 us -> none  [per_device(): (mixed + lax.psum(mlp_term.astype(bf16), 'tensor').astype(f32)).astype(bf16)]
    slice x0 -> x1, local copies, waits for them, and re-layouts: none -> 3.12 us  [per_device(): return layer(qkv, post_gain[None, :], tokens, w_out, w_up, w_down)[:ROWS]]
  transfers between devices with their start and end apart: 2 -> 0, of which waited for: 1 -> 0; matrix products, arithmetic and copies ran while one was open for 2% -> 0% of each run, Pallas kernels for 51% -> 0%
where the time goes in v2:
time: 152 us
  Pallas kernels  141 us (93%)
  local copies, waits for them, and re-layouts  6.88 us (5%)
  other arithmetic  2.71 us (2%)
  matrix products  1.67 us (1%)
    pallas_call x1, Pallas kernels, layer(): pl.pallas_call(layer_kernel, out_shape=jax.ShapeDtypeStruct((PAD, D), bf1...  141 us
    slice x1, local copies, waits for them, and re-layouts, per_device(): return layer(qkv, post_gain[None, :], tokens, w_out, w_up, w_down)[:ROWS]  3.12 us

profile of v2, /device:TPU:0, one launch (start us, length us, event | category | flops | bytes accessed | tf_op | source)
XLA Modules:
  0.0 152.1 jit_solution(5531298620224369760)
XLA Ops:
  0.0 0.0 copy-start
  0.0 0.0 copy-start.4
  0.0 0.0 copy-start.1
  0.0 0.0 copy-start.2
  0.0 2.1 %copy-done = bf16[1536,3,192]{0,2,1:T(8,128)(2,1)S(1)} copy-done((bf16[1536,3,192]{0,2,1:T(8,128)(2,1)S(1)}, bf16[1536,3,192]{0,2,1:T(8,128)(2,1)}, u32[]{:S(2)}) %copy-start) | copy-done | bytes 1769496
  2.2 0.0 copy-start.3
  2.2 2.0 %convert_reduce_fusion = f32[720]{0:T(1024)S(1)} fusion(bf16[720,1536]{1,0:T(8,128)(2,1)} %tokens.1), kind=kLoop, calls=%fused_computation.1 | loop fusion | flops 2211120 | bytes 2214720 | tf_op jit(solution)/shard_map/reduce_sum | solution.py:33
  4.2 0.0 copy-done.1
  4.2 0.7 fusion.2
  4.9 0.0 copy-done.2
  4.9 0.6 broadcast_in_dim.2.gain
  5.5 0.0 copy-done.4
  5.5 0.0 copy-done.3
  5.5 1.7 %fusion.12 = bf16[576,720]{1,0:T(8,128)(2,1)S(1)} fusion(bf16[1536,576]{0,1:T(8,128)(2,1)S(1)} %bitcast.5, bf16[720,1536]{1,0:T(8,128)(2,1)S(1)} %copy-done.1, f32[1536]{0:T(1024)S(1)} %copy-done.3, f32[720]{0:T(1024)S(1)} %add_rsqrt_fusion, f32[720]{0:T(1024)S(1)} %broadcast_multiply_fusion, f32[576]{0:T(1024)S(1)} %copy-done.4), kind=kOutput, calls=%fused_computation.12 | convolution fusion | flops 1280378880 | bytes 4824960 | tf_op jit(solution)/shard_map/dot_general | solution.py:555
  7.2 1.0 pad.4
  8.2 140.8 %layer.1 = bf16[768,1536]{1,0:T(8,128)(2,1)} custom-call(bf16[3,4,48,768]{3,2,1,0:T(8,128)(2,1)} %bitcast.6, f32[1,1536]{1,0:T(1,128)} %broadcast_in_dim.2.gain, bf16[720,1536]{1,0:T(8,128)(2,1)} %tokens.1, bf16[192,1536]{1,0:T(8,128)(2,1)} %w_out.1, bf16[1536,768]{1,0:T(8,128)(2,1)} %w_up.1, bf16[768,1536]{1,0:T(8,128)(2,1)} %w_down.1), custom_call_target="tpu_custom_call" | custom-call | flops 60000002048 | bytes 4000000 | tf_op jit(solution)/shard_map/layer/pallas_call | solution.py:503
  149.0 3.1 %slice.3 = bf16[720,1536]{1,0:T(8,128)(2,1)} slice(bf16[768,1536]{1,0:T(8,128)(2,1)} %layer.1), slice={[0:720], [0:1536]} | slice | bytes 4423680 | tf_op jit(solution)/shard_map/slice | solution.py:558
  (2 shorter events, 0.0 us)
Async XLA Ops:
  0.0 2.2 %copy-start = (bf16[1536,3,192]{0,2,1:T(8,128)(2,1)S(1)}, bf16[1536,3,192]{0,2,1:T(8,128)(2,1)}, u32[]{:S(2)}) copy-start(bf16[1536,3,192]{0,2,1:T(8,128)(2,1)} %param.9) | copy-start | bytes 5308420
  0.0 5.5 %copy-start.4 = (f32[576]{0:T(1024)S(1)}, f32[576]{0:T(1024)}, u32[]{:S(2)}) copy-start(f32[576]{0:T(1024)} %constant.12.clone.1) | copy-start | bytes 6916
  0.0 4.2 %copy-start.1 = (bf16[720,1536]{1,0:T(8,128)(2,1)S(1)}, bf16[720,1536]{1,0:T(8,128)(2,1)}, u32[]{:S(2)}) copy-start(bf16[720,1536]{1,0:T(8,128)(2,1)} %tokens.1) | copy-start | bytes 6635524
  0.0 4.9 %copy-start.2 = (f32[1536]{0:T(1024)S(1)}, f32[1536]{0:T(1024)}, u32[]{:S(2)}) copy-start(f32[1536]{0:T(1024)} %param.11) | copy-start | bytes 18436
  2.2 3.4 %copy-start.3 = (f32[1536]{0:T(1024)S(1)}, f32[1536]{0:T(1024)}, u32[]{:S(2)}) copy-start(f32[1536]{0:T(1024)} %param.8) | copy-start | bytes 18436

commit v3 on v2

--- a/solution.py
+++ b/solution.py
@@ -21,12 +21,12 @@
 OWN, A, B, C, F, D, E, G = range(8)
 DZ = (0, 0, 0, 1, 0, 1, 1, 1)
 DY = (0, 3, 1, 0, 2, 3, 1, 2)
-ORDER = (
-    (OWN, 0), (OWN, 1), (A, 0), (B, 0), (C, 0), (A, 1), (B, 1), (C, 1),
-    (F, 0), (F, 1), (D, 0), (E, 0), (D, 1), (E, 1), (G, 0), (G, 1),
-)
-ARRIVE = {0: ((OWN, 1),), 1: ((A, 0), (B, 0), (C, 0)), 4: ((A, 1),), 5: ((B, 1),), 6: ((C, 1),), 7: ((F, 0),), 8: ((F, 1),),
-          9: ((D, 0), (E, 0)), 11: ((D, 1),), 12: ((E, 1),), 13: ((G, 0),), 14: ((G, 1),)}
+ARRIVE = {
+    0: ((0, OWN, 1),), 1: ((0, A, 0), (0, B, 0), (0, C, 0)), 4: ((0, A, 1),), 5: ((0, B, 1),), 6: ((0, C, 1), (0, D, 0), (0, E, 0)),
+       9: ((0, D, 1),), 10: ((0, E, 1),), 11: ((0, F, 0),), 12: ((0, G, 0),), 13: ((0, F, 1),),
+    14: ((0, G, 1),), 15: ((1, OWN, 1),), 16: ((1, A, 0), (1, B, 0), (1, C, 0)), 20: ((1, A, 1),), 21: ((1, B, 1), (1, D, 0), (1, E, 0)),
+    22: ((1, C, 1),), 23: ((1, D, 1),), 24: ((1, E, 1), (1, F, 0)), 25: ((1, G, 0), (1, F, 1)), 26: ((1, G, 1),),
+}
 
 
 def layer_norm(values, gain):
@@ -53,12 +53,16 @@
     seq_near = [seq_id(OWN, 1), seq_id(A), seq_id(B), seq_id(C)]
     ten_near = [ten_id(0, 1), ten_id(0, 3), ten_id(1, 0), ten_id(1, 1), ten_id(1, 3)]
     ten_all = [ten_id(0, 1), ten_id(0, 3), ten_id(0, 2), ten_id(1, 0), ten_id(1, 1), ten_id(1, 3)]
-    own_rows = pl.ds(pl.multiple_of(ti * 192, 16), 192)
     loads = [
-        pltpu.make_async_copy(w_out, wf.at[own_rows], lsem.at[0]),
-        pltpu.make_async_copy(w_up, wu, lsem.at[1]),
-        pltpu.make_async_copy(w_down, wd, lsem.at[2]),
-        pltpu.make_async_copy(tokens, tok.at[0:ROWS], lsem.at[3]),
+        pltpu.make_async_copy(w_up, wu, lsem.at[0]),
+        pltpu.make_async_copy(w_down, wd, lsem.at[1]),
+        pltpu.make_async_copy(tokens, tok.at[0:ROWS], lsem.at[2]),
+    ]
+    loads += [
+        pltpu.make_async_copy(
+            w_out.at[h * HD : (h + 1) * HD], wf.at[pl.ds(pl.multiple_of(h * 384 + ti * HD, 16), HD)], lsem.at[3 + h]
+        )
+        for h in range(4)
     ]
     for c in loads:
         c.start()
@@ -81,10 +85,11 @@
     for h in range(4):
         kt[me, h] = qkv[1, h]
         vt[me, h, 0:HD, :] = qkv[2, h]
-    peak[...] = jnp.full(peak.shape, -1e30, f32)
+    peak[0:4] = jnp.full((4, 16, PAD), -1e30, f32)
+    peak[4:6] = jnp.ones((2, 16, PAD), f32)
     acc[...] = jnp.zeros(acc.shape, f32)
     p0[ROWS:PAD, :] = jnp.zeros((PAD - ROWS, PAD), bf16)
-    p1[ROWS:PAD, :] = jnp.zeros((PAD - ROWS, PAD), bf16)
+    p1[...] = jnp.zeros((PAD, PAD), bf16)
     tok[ROWS:PAD, :] = jnp.zeros((PAD - ROWS, 1536), bf16)
     pl.semaphore_wait(barrier, len(seq_near) + len(ten_all))
 
@@ -117,23 +122,29 @@
             seq_copy(piece, slot, hp, me, 0).wait_recv()
         if other:
             return
-        if off in (A, D):
-            send(0, slot, hp, seq_id(B))
-        if off in (B, E):
-            send(1, slot, hp, seq_id(A))
+        if off in (D, E):
+            onward(hp, off)
         for piece in (0, 1):
             send(piece, slot, hp, seq_id(OWN, 1))
+
+    def onward(hp, off):
+        if off in (A, D):
+            send(0, seq_id(off), hp, seq_id(B))
+        else:
+            send(1, seq_id(off), hp, seq_id(A))
 
     def spread(hp):
         slot = seq_id(C)
         for piece in (0, 1):
             for d in (seq_id(B), seq_id(A)):
                 send(piece, slot, hp, d)
+        onward(hp, A)
+        onward(hp, B)
 
     tsent = []
 
     def head_ref(src, head):
-        return att.at[pl.ds(pl.multiple_of(src * 192 + head * HD, 16), HD)]
+        return att.at[pl.ds(pl.multiple_of(head * 384 + src * HD, 16), HD)]
 
     def ten_copy(src, head, dest, index):
         return pltpu.make_async_remote_copy(
@@ -146,36 +157,30 @@
         c.start()
         tsent.append(0)
 
-    def finish(hp):
-        for h in (2 * hp, 2 * hp + 1):
-            att[pl.ds(pl.multiple_of(ti * 192 + h * HD, 16), HD), :] = (acc[h, 0:HD, :] / acc[h, HD : HD + 1, :]).astype(bf16)
-        for h in (2 * hp, 2 * hp + 1):
+    def finish(heads):
+        for h in heads:
+            att[pl.ds(pl.multiple_of(h * 384 + ti * HD, 16), HD), :] = (acc[h, 0:HD, :] / acc[h, HD : HD + 1, :]).astype(bf16)
+        for h in heads:
             for d in ten_near:
                 ten_start(ti, h, d)
 
     def ten_wait(src, head):
         ten_copy(src, head, ti, 0).wait_recv()
 
-    def relay(hp):
-        for dz in (0, 1):
-            left, right = ten_id(dz, 3), ten_id(dz, 1)
-            for h in (2 * hp, 2 * hp + 1):
-                ten_wait(left, h)
-                ten_wait(right, h)
-            ten_start(left, 2 * hp, ten_id(0, 1))
-            ten_start(right, 2 * hp + 1, ten_id(0, 3))
-
-    def collect(hp):
-        for h in (2 * hp, 2 * hp + 1):
-            ten_wait(ten_id(1, 0), h)
-            ten_wait(ten_id(0, 2), h)
-            ten_wait(ten_id(1, 2), h)
+    def relay(head):
+        for src, dest in ((ten_id(0, 3), ten_id(0, 1)), (ten_id(1, 1), ten_id(0, 3))):
+            ten_wait(src, head)
+            ten_start(src, head, dest)
+
+    def collect(head):
+        for src in (ten_id(0, 1), ten_id(1, 3), ten_id(1, 0), ten_id(0, 2), ten_id(1, 2)):
+            ten_wait(src, head)
 
     wsent = []
 
     def w_copy(src, half, other, dest, index):
         at = lax.rem(core + other, 2)
-        ref = wf.at[pl.ds(pl.multiple_of(src * 192 + at * 96 + half * 48, 16), 48)]
+        ref = wf.at[pl.ds(pl.multiple_of((at * 2 + half) * 384 + src * HD, 16), HD)]
         return pltpu.make_async_remote_copy(
             src_ref=ref, dst_ref=ref, send_sem=wsend.at[index], recv_sem=wrecv.at[src, other, half],
             device_id=dest, device_id_type=MESH,
@@ -183,7 +188,7 @@
 
     def w_start(src, half, dest, index_other=0):
         at = core
-        ref = wf.at[pl.ds(pl.multiple_of(src * 192 + at * 96 + half * 48, 16), 48)]
+        ref = wf.at[pl.ds(pl.multiple_of((at * 2 + half) * 384 + src * HD, 16), HD)]
         pltpu.make_async_remote_copy(
             src_ref=ref, dst_ref=ref, send_sem=wsend.at[len(wsent)], recv_sem=wrecv.at[src, index_other, half],
             device_id=dest, device_id_type=MESH,
@@ -198,7 +203,8 @@
             w_start(src, half, {"seq": seq_id(OWN, 1)}, 1)
 
     def w_own():
-        loads[0].wait()
+        for c in loads[3:]:
+            c.wait()
         for half in (0, 1):
             for d in (ten_id(0, 1), ten_id(0, 3), ten_id(1, 0)):
                 w_start(ti, half, {"tensor": d})
@@ -237,11 +243,14 @@
     S, Pw = (s0, s1), (p0, p1)
 
     def slot_at(pos):
-        code = pos * 0
-        for j, (off, other) in enumerate(ORDER):
-            code = code + (pos == j).astype(jnp.int32) * (DZ[off] * 8 + DY[off] * 2 + other)
-        dz, dy, dc = lax.div(code, 8), lax.rem(lax.div(code, 2), 4), lax.rem(code, 2)
-        return (lax.rem(zh + dz, 2) * 4 + lax.rem(yy + dy, 4)) * 2 + lax.rem(core + dc, 2)
+        mid, late = (pos >= 2).astype(jnp.int32), (pos >= 8).astype(jnp.int32)
+        q, r = lax.rem(pos + 4, 6), lax.rem(pos, 4)
+        chip = mid * (1 - late) * (1 + lax.rem(q, 3)) + late * (2 * lax.div(pos, 4) + lax.rem(r, 2))
+        other = (1 - mid) * pos + mid * (1 - late) * lax.div(q, 3) + late * lax.div(r, 2)
+        far = (chip >= 6).astype(jnp.int32)
+        dy = (1 - far) * lax.rem(3 * lax.rem(chip, 3), 5) + 2 * far
+        dz = (1 - far) * lax.div(chip, 3) + far * (chip - 6)
+        return (lax.rem(zh + dz, 2) * 4 + lax.rem(yy + dy, 4)) * 2 + lax.rem(core + other, 2)
 
     def score_pieces(slot, head, par, top):
         def mk(c, half):
@@ -298,74 +307,80 @@
         for c in range(NC):
             peak[head, 8:16, c * W : (c + 1) * W] = top[c]
 
-    def step(t, _):
-        for hp in (0, 1):
-            for j, blocks in ARRIVE.items():
-
-                @pl.when(t == 16 * hp + j)
-                def _(hp=hp, j=j, blocks=blocks):
-                    for off, other in blocks:
-                        arrive(hp, off, other)
-                    if j == 1:
-                        spread(hp)
-                    if j == 9 and hp == 0:
-                        send_own(1)
-
-        @pl.when(t == 5)
-        def _():
-            w_cross()
-            w_relay(0)
-
-        @pl.when(t == 12)
-        def _():
-            w_relay(1)
-            w_far(0)
-
-        @pl.when(t == 15)
-        def _():
-            w_far(1)
-
-        @pl.when(t == 16)
-        def _():
-            finish(0)
-
-        @pl.when(t == 22)
-        def _():
-            relay(0)
-
-        @pl.when(t == 28)
-        def _():
-            collect(0)
-            w_collect()
-
-        hp = lax.div(t, 16)
-        slot = slot_at(lax.rem(t, 16))
-        nxt = lax.rem(t + 1, 32)
-        slot_next = slot_at(lax.rem(nxt, 16))
-        held = None
+    def item(n):
+        n = lax.rem(n, 64)
+        late = (n >= 44).astype(jnp.int32)
+        last = (n >= 54).astype(jnp.int32)
+        pos = (1 - late) * lax.div(lax.rem(n, 32), 2) + late * (n - 38 - 10 * last)
+        head = (1 - late) * (2 * lax.div(n, 32) + lax.rem(n, 2)) + late * (2 + last)
+        return slot_at(pos), head
+
+    def step(t, held):
+        def events(at):
+            for hp, off, other in ARRIVE.get(at, ()):
+                arrive(hp, off, other)
+            if at == 1:
+                spread(0)
+            if at == 5:
+                w_cross()
+                w_relay(0)
+            if at == 7:
+                send_own(1)
+            if at == 12:
+                w_relay(1)
+                w_far(0)
+            if at == 15:
+                w_far(1)
+            if at == 16:
+                spread(1)
+            if at == 17:
+                finish((0, 1))
+            if at == 24:
+                relay(0)
+                relay(1)
+            if at == 30:
+                collect(0)
+                collect(1)
+                w_collect()
+            if at == 28:
+                finish((2,))
+
+        at_all = sorted(set(ARRIVE) | {1, 5, 7, 12, 15, 16, 17, 24, 28, 30})
+
+        def search(lo, hi):
+            inside = [at for at in at_all if lo <= at < hi]
+            if not inside:
+                return
+            if hi - lo == 1:
+                events(lo)
+                return
+            mid = (lo + hi) // 2
+            for a, b in ((lo, mid), (mid, hi)):
+                if any(a <= at < b for at in inside):
+                    test = t < mid if a == lo else t >= mid
+                    pl.when(test)(functools.partial(search, a, b))
+
+        search(0, 32)
+        slots = {q: item(2 * t + q) for q in (1, 2)}
+        slots[-1], slots[0] = (held[0], held[1]), (held[2], held[3])
         for k in (0, 1):
-            head = 2 * hp + k
-            now, factor = {}, {}
+            (slot_p, head_p), (slot, head), (slot_n, head_n) = slots[k - 1], slots[k], slots[k + 1]
+            now, factor_p = {}, {}
             for c in range(NC):
                 cs = slice(c * W, (c + 1) * W)
+                factor_p[c] = peak[5 - k, 0:1, cs]
                 old = peak[head, 0:1, cs]
                 now[c] = jnp.maximum(old, jnp.max(peak[head, 8:16, cs], axis=0, keepdims=True))
-                factor[c] = jnp.exp2(old - now[c])
+                peak[4 + k, 0:1, cs] = jnp.exp2(old - now[c])
                 peak[head, 0:1, cs] = now[c]
-            head_n = head + 1 if k == 0 else 2 * lax.div(nxt, 16)
-            slot_n = slot if k == 0 else slot_next
             top = {}
-            scores = score_pieces(slot_n, head_n, 1 - k, top)
-            weights = weight_pieces(k, now)
-            if held is None:
-                interleave(scores, weights)
-                held = value_pieces(slot, head, k, factor)
-            else:
-                interleave(scores, weights, held)
-                for x in value_pieces(slot, head, k, factor):
-                    x()
+            interleave(
+                score_pieces(slot_n, head_n, 1 - k, top),
+                weight_pieces(k, now),
+                value_pieces(slot_p, head_p, 1 - k, factor_p),
+            )
             keep_top(head_n, top)
-        return 0
+        return (*slots[1], *slots[2])
 
     send_own(0)
     w_own()
@@ -373,23 +388,36 @@
     for x in score_pieces(me, 0, 0, top):
         x()
     keep_top(0, top)
-    lax.fori_loop(0, 32, step, 0)
-    finish(1)
-    relay(1)
-    collect(1)
-    for c in loads[1:]:
+    lax.fori_loop(0, 32, step, (me, me * 0, me, me * 0))
+    for x in value_pieces(slot_at(me * 0 + 15), 3, 1, {c: peak[5, 0:1, c * W : (c + 1) * W] for c in range(NC)}):
+        x()
+    finish((3,))
+    relay(2)
+    for c in loads[:3]:
         c.wait()
 
     def project(c, _):
         cols = pl.ds(pl.multiple_of(c * W, W), W)
-        m = tok[cols, :].astype(f32) + lax.dot_general(
-            att[:, cols], wf[...], (((0,), (0,)), ((), ())), preferred_element_type=f32
+        mixed[cols, :] = tok[cols, :].astype(f32) + lax.dot_general(
+            att[0:768, cols], wf[0:768, :], (((0,), (0,)), ((), ())), preferred_element_type=f32
+        )
+        return 0
+
+    lax.fori_loop(0, NC, project, 0)
+    relay(3)
+    collect(2)
+    collect(3)
+
+    def complete(c, _):
+        cols = pl.ds(pl.multiple_of(c * W, W), W)
+        m = mixed[cols, :] + lax.dot_general(
+            att[768:1536, cols], wf[768:1536, :], (((0,), (0,)), ((), ())), preferred_element_type=f32
         )
         mixed[cols, :] = m
         post[cols, :] = layer_norm(m, gain[...]).astype(bf16)
         return 0
 
-    lax.fori_loop(0, NC, project, 0)
+    lax.fori_loop(0, NC, complete, 0)
 
     def rows_of(t, half=0, n=48):
         return pl.ds(pl.multiple_of(t * 96 + half * 48, 16), n)
@@ -513,7 +541,7 @@
             pltpu.VMEM((PAD, PAD), bf16),
             pltpu.VMEM((PAD, PAD), bf16),
             pltpu.VMEM((4, 64, PAD), f32),
-            pltpu.VMEM((4, 16, PAD), f32),
+            pltpu.VMEM((6, 16, PAD), f32),
             pltpu.VMEM((D, PAD), bf16),
             pltpu.VMEM((D, D), bf16),
             pltpu.VMEM((PAD, D), bf16),
@@ -534,7 +562,7 @@
             pltpu.SemaphoreType.DMA((NTEN, 4)),
             pltpu.SemaphoreType.DMA((32,)),
             pltpu.SemaphoreType.DMA((NTEN, 2, 2)),
-            pltpu.SemaphoreType.DMA((4,)),
+            pltpu.SemaphoreType.DMA((7,)),
             pltpu.SemaphoreType.DMA((16,)),
             pltpu.SemaphoreType.DMA((2, 3)),
             pltpu.SemaphoreType.DMA((4,)),

time: 152 us -> 139 us (0.914)
  Pallas kernels: 141 us -> 127 us
    pallas_call x1, Pallas kernels: 141 us -> 127 us  [layer(): pl.pallas_call(layer_kernel, out_shape=jax.ShapeDtypeStruct((PAD, D), bf1...]
where the time goes in v3:
time: 139 us
  Pallas kernels  127 us (91%)
  local copies, waits for them, and re-layouts  6.88 us (5%)
  other arithmetic  2.71 us (2%)
  matrix products  1.67 us (1%)
    pallas_call x1, Pallas kernels, layer(): pl.pallas_call(layer_kernel, out_shape=jax.ShapeDtypeStruct((PAD, D), bf1...  127 us
    slice x1, local copies, waits for them, and re-layouts, per_device(): return layer(qkv, post_gain[None, :], tokens, w_out, w_up, w_down)[:ROWS]  3.12 us

profile of v3, /device:TPU:0, one launch (start us, length us, event | category | flops | bytes accessed | tf_op | source)
XLA Modules:
  0.0 138.7 jit_solution(9588125850489830594)
XLA Ops:
  0.0 0.0 copy-start
  0.0 0.0 copy-start.4
  0.0 0.0 copy-start.1
  0.0 0.0 copy-start.2
  0.0 2.1 %copy-done = bf16[1536,3,192]{0,2,1:T(8,128)(2,1)S(1)} copy-done((bf16[1536,3,192]{0,2,1:T(8,128)(2,1)S(1)}, bf16[1536,3,192]{0,2,1:T(8,128)(2,1)}, u32[]{:S(2)}) %copy-start) | copy-done | bytes 1769496
  2.2 0.0 copy-start.3
  2.2 2.0 %convert_reduce_fusion = f32[720]{0:T(1024)S(1)} fusion(bf16[720,1536]{1,0:T(8,128)(2,1)} %tokens.1), kind=kLoop, calls=%fused_computation.1 | loop fusion | flops 2211120 | bytes 2214720 | tf_op jit(solution)/shard_map/reduce_sum | solution.py:33
  4.2 0.0 copy-done.1
  4.2 0.7 fusion.2
  4.9 0.0 copy-done.2
  4.9 0.6 broadcast_in_dim.2.gain
  5.5 0.0 copy-done.4
  5.5 0.0 copy-done.3
  5.5 1.7 %fusion.12 = bf16[576,720]{1,0:T(8,128)(2,1)S(1)} fusion(bf16[1536,576]{0,1:T(8,128)(2,1)S(1)} %bitcast.5, bf16[720,1536]{1,0:T(8,128)(2,1)S(1)} %copy-done.1, f32[1536]{0:T(1024)S(1)} %copy-done.3, f32[720]{0:T(1024)S(1)} %add_rsqrt_fusion, f32[720]{0:T(1024)S(1)} %broadcast_multiply_fusion, f32[576]{0:T(1024)S(1)} %copy-done.4), kind=kOutput, calls=%fused_computation.12 | convolution fusion | flops 1280378880 | bytes 4824960 | tf_op jit(solution)/shard_map/dot_general | solution.py:583
  7.2 1.0 pad.4
  8.2 127.4 %layer.1 = bf16[768,1536]{1,0:T(8,128)(2,1)} custom-call(bf16[3,4,48,768]{3,2,1,0:T(8,128)(2,1)} %bitcast.6, f32[1,1536]{1,0:T(1,128)} %broadcast_in_dim.2.gain, bf16[720,1536]{1,0:T(8,128)(2,1)} %tokens.1, bf16[192,1536]{1,0:T(8,128)(2,1)} %w_out.1, bf16[1536,768]{1,0:T(8,128)(2,1)} %w_up.1, bf16[768,1536]{1,0:T(8,128)(2,1)} %w_down.1), custom_call_target="tpu_custom_call" | custom-call | flops 60000002048 | bytes 4000000 | tf_op jit(solution)/shard_map/layer/pallas_call | solution.py:531
  135.6 3.1 %slice.3 = bf16[720,1536]{1,0:T(8,128)(2,1)} slice(bf16[768,1536]{1,0:T(8,128)(2,1)} %layer.1), slice={[0:720], [0:1536]} | slice | bytes 4423680 | tf_op jit(solution)/shard_map/slice | solution.py:586
  (2 shorter events, 0.0 us)
Async XLA Ops:
  0.0 2.2 %copy-start = (bf16[1536,3,192]{0,2,1:T(8,128)(2,1)S(1)}, bf16[1536,3,192]{0,2,1:T(8,128)(2,1)}, u32[]{:S(2)}) copy-start(bf16[1536,3,192]{0,2,1:T(8,128)(2,1)} %param.9) | copy-start | bytes 5308420
  0.0 5.5 %copy-start.4 = (f32[576]{0:T(1024)S(1)}, f32[576]{0:T(1024)}, u32[]{:S(2)}) copy-start(f32[576]{0:T(1024)} %constant.12.clone.1) | copy-start | bytes 6916
  0.0 4.2 %copy-start.1 = (bf16[720,1536]{1,0:T(8,128)(2,1)S(1)}, bf16[720,1536]{1,0:T(8,128)(2,1)}, u32[]{:S(2)}) copy-start(bf16[720,1536]{1,0:T(8,128)(2,1)} %tokens.1) | copy-start | bytes 6635524
  0.0 4.9 %copy-start.2 = (f32[1536]{0:T(1024)S(1)}, f32[1536]{0:T(1024)}, u32[]{:S(2)}) copy-start(f32[1536]{0:T(1024)} %param.11) | copy-start | bytes 18436
  2.2 3.4 %copy-start.3 = (f32[1536]{0:T(1024)S(1)}, f32[1536]{0:T(1024)}, u32[]{:S(2)}) copy-start(f32[1536]{0:T(1024)} %param.8) | copy-start | bytes 18436
